TPU v7x, 32 devices: a whole 2x2x4 slice. The times are simulated.
32 devices in a mesh: dp: 4 (over x, core), mp: 8 (over z, y).
Axes of the slice: x: 2, y: 2, z: 4, core: 2. Of those that a mesh axis runs over, the one named last changes fastest.
Arguments:
- attn_out: bfloat16 [512, 8192], P('dp', 'mp'), may hold values from -6 to 6
- residual: bfloat16 [512, 8192], P('dp', 'mp'), may hold values from -40 to 40
- output_weight: bfloat16 [8192, 8192], P('mp', 'dp'), may hold values from -0.0625 to 0.0625
- prune_mask: int32 [8192, 128], P('mp'), may hold values 0 or 1
- inverse_factor: float32 [128, 8192], P(None, 'dp'), may hold values from -2 to 2, as said below
- norm_gain: bfloat16 [8192], P('mp'), may hold values from 0.5 to 1.5
- gate_up_weight: bfloat16 [8192, 2, 14336], P('dp', None, 'mp'), may hold values from -0.0625 to 0.0625
Outputs:
- pruned_weight: bfloat16 [8192, 8192], P('mp', 'dp')
- stream: bfloat16 [512, 8192], P('dp', 'mp')
- hessian: float32 [14336, 14336], P('mp', 'dp')
Inputs may be any that keep to these rules, and one draw needn't show every extreme that they name: inverse_factor is zero below its diagonal, and its diagonal lies between 0.5 and 2.
All inputs are finite; a program needn't handle non-finite values. No bound on the sum of `prune_mask` on one device may be relied on, other than what follows from the above.
Results may differ from a plain program's by a relative error of at most 0.012.
Values may be sent and summed in bfloat16 or wider, within the bound.
A program may use at most 128 MiB of HBM per device.

v0:
```python
import jax
import jax.numpy as jnp
from jax import lax
from jax.sharding import PartitionSpec as P


def from_root(block, axis, holder):
    block = jnp.where(lax.axis_index(axis) == holder, block, jnp.zeros_like(block))
    return lax.psum(block, axis)


def body(attn_out, residual, output_weight, prune_mask, inverse_factor, norm_gain, gate_up_weight):
    width_block = prune_mask.shape[1]
    kept_mask = prune_mask.astype(jnp.float32)
    weight_cols = output_weight.astype(jnp.float32)
    is_first = lax.axis_index("dp") == 0
    factor_block = inverse_factor[:, :width_block]
    pivots = jnp.where(is_first, jnp.diagonal(factor_block), 1.0)
    cutting = (1.0 - kept_mask) / pivots[None, :]
    sub_width = min(32, width_block)
    strict = jnp.tril(jnp.ones((sub_width, sub_width), jnp.float32), -1)
    identity_sub = jnp.eye(sub_width, dtype=jnp.float32)[None, :, :]
    pieces = []
    for begin in range(0, width_block, sub_width):
        current = weight_cols[:, begin : begin + sub_width]
        if begin > 0:
            earlier = jnp.concatenate(pieces, axis=1)
            current = current - jnp.dot(
                earlier,
                factor_block[:begin, begin : begin + sub_width],
                precision=lax.Precision.HIGHEST,
                preferred_element_type=jnp.float32,
            )
        cut_part = cutting[:, begin : begin + sub_width]
        inner = factor_block[begin : begin + sub_width, begin : begin + sub_width]
        system = cut_part[:, :, None] * (inner.T * strict)[None, :, :] + identity_sub
        target = (cut_part * current)[:, :, None]
        pieces.append(
            jax.scipy.linalg.solve_triangular(system, target, lower=True, unit_diagonal=True)[
                :, :, 0
            ]
        )
    solved = jnp.concatenate(pieces, axis=1)
    errors = from_root(solved, "dp", 0)
    updated = weight_cols - jnp.dot(
        errors, inverse_factor, precision=lax.Precision.HIGHEST, preferred_element_type=jnp.float32
    )
    leading = jnp.where(is_first, updated[:, :width_block] * kept_mask, updated[:, :width_block])
    pruned_weight = lax.dynamic_update_slice_in_dim(updated, leading, 0, 1).astype(jnp.bfloat16)
    features = lax.all_gather(attn_out, "mp", axis=1, tiled=True)
    projected = lax.dot_general(
        features,
        lax.all_gather(pruned_weight, "dp", axis=1, tiled=True),
        (((1,), (1,)), ((), ())),
        preferred_element_type=jnp.float32,
    )
    stream = (residual.astype(jnp.float32) + projected).astype(jnp.bfloat16)
    width_model = features.shape[1]
    stream_float = stream.astype(jnp.float32)
    squares = lax.psum(jnp.sum(stream_float * stream_float, axis=1), "mp")
    inverse = lax.rsqrt(squares / width_model + 1e-05)
    normed = (stream_float * inverse[:, None] * norm_gain.astype(jnp.float32)[None, :]).astype(
        jnp.bfloat16
    )
    normed_all = lax.all_gather(normed, "mp", axis=1, tiled=True)
    input_rows = gate_up_weight.shape[0]
    unit_count = gate_up_weight.shape[2]
    slices = lax.all_to_all(normed_all, "dp", split_axis=1, concat_axis=0, tiled=True)
    flat_weight = gate_up_weight.reshape(input_rows, 2 * unit_count)
    gate_up = lax.psum_scatter(
        jnp.dot(slices, flat_weight, preferred_element_type=jnp.float32),
        "dp",
        scatter_dimension=0,
        tiled=True,
    )
    gate_part = gate_up[:, :unit_count]
    up_part = gate_up[:, unit_count:]
    hidden = (jax.nn.silu(gate_part) * up_part).astype(jnp.bfloat16)
    hidden_all = lax.all_gather(hidden, "mp", axis=1, tiled=True)
    count_rows = hidden_all.shape[1] // lax.axis_size("mp")
    window_local = lax.dynamic_slice_in_dim(
        hidden_all, lax.axis_index("mp") * count_rows, count_rows, 1
    )
    weighting = 2.0 / (hidden_all.shape[0] * lax.axis_size("dp"))
    contract = (((0,), (0,)), ((), ()))
    columns = lax.all_to_all(hidden_all, "dp", split_axis=1, concat_axis=0, tiled=True)
    window_all = lax.all_gather(window_local, "dp", axis=0, tiled=True)
    hessian = weighting * lax.dot_general(
        window_all, columns, contract, preferred_element_type=jnp.float32
    )
    return (pruned_weight, stream, hessian)


def solution(mesh):
    in_specs = (
        P("dp", "mp"),
        P("dp", "mp"),
        P("mp", "dp"),
        P("mp", None),
        P(None, "dp"),
        P("mp"),
        P("dp", None, "mp"),
    )
    out_specs = (P("mp", "dp"), P("dp", "mp"), P("mp", "dp"))
    return jax.shard_map(body, mesh=mesh, in_specs=in_specs, out_specs=out_specs, check_vma=False)
```

profile of v0, /device:TPU:0, one launch (start us, length us, event | category | flops | bytes accessed | tf_op | source)
XLA Modules:
  0.0 952.4 jit_solution(11305181622557403256)
XLA Ops:
  10.3 6.4 copy.20
  16.7 6.7 convert_element_type.40
  26.0 7.3 add_bitcast_fusion.3
  33.3 100.7 %custom-call.8 = f32[1024,1,32,32]{0,2,3,1:T(8,128)} custom-call(f32[1024,1,32,32]{0,3,2,1:T(8,128)} %get-tuple-element.19), custom_call_target="InvertDiagBlocksLowerTriangular" | custom-call | tf_op jit(solution)/shard_map/jit(_solve_triangular)/vmap()/triangular_solve | solution.py:39
  134.0 2.7 fusion.3
  138.0 100.7 %custom-call.9 = f32[1024,1,32,32]{0,2,3,1:T(8,128)} custom-call(f32[1024,1,32,32]{0,3,2,1:T(8,128)} %get-tuple-element.20), custom_call_target="InvertDiagBlocksLowerTriangular" | custom-call | tf_op jit(solution)/shard_map/jit(_solve_triangular)/vmap()/triangular_solve | solution.py:39
  238.7 2.7 fusion.2
  242.7 100.6 %custom-call.10 = f32[1024,1,32,32]{0,2,3,1:T(8,128)} custom-call(f32[1024,1,32,32]{0,3,2,1:T(8,128)} %get-tuple-element.21), custom_call_target="InvertDiagBlocksLowerTriangular" | custom-call | tf_op jit(solution)/shard_map/jit(_solve_triangular)/vmap()/triangular_solve | solution.py:39
  343.3 2.7 fusion.1
  347.4 100.6 %custom-call.11 = f32[1024,1,32,32]{0,2,3,1:T(8,128)} custom-call(f32[1024,1,32,32]{0,3,2,1:T(8,128)} %get-tuple-element.22), custom_call_target="InvertDiagBlocksLowerTriangular" | custom-call | tf_op jit(solution)/shard_map/jit(_solve_triangular)/vmap()/triangular_solve | solution.py:39
  448.0 2.7 fusion
  452.4 35.5 %all-reduce.2.cloned.1.call-done = f32[1024,128]{0,1:T(8,128)} async-done(((f32[1024,128]{0,1:T(8,128)}), f32[1024,128]{0,1:T(8,128)}) %all-reduce.2.cloned.1.call-update) | async-done | bytes 524304 | tf_op jit(solution)/shard_map/psum | solution.py:9
  487.8 12.2 %convolution_subtract_fusion = f32[1024,2048]{0,1:T(8,128)S(1)} fusion(f32[1024,128]{0,1:T(8,128)} %all-reduce.2.cloned.1.call-done, f32[128,2048]{1,0:T(8,128)S(1)} %copy-done, bf16[1024,2048]{0,1:T(8,128)(2,1)} %copy.20), kind=kOutput, calls=%fused_computation.2 | convolution fusion | flops 3225419776 | bytes 14155776 | tf_op jit(solution)/shard_map/dot_general | solution.py:45
  500.2 2.6 convert_element_type.43
  504.0 1.9 all-gather.8.cloned.1.call-done
  505.9 105.8 %all-gather.6.cloned.1.call-done = bf16[1024,8192]{0,1:T(8,128)(2,1)} async-done(((bf16[1024,2048]{0,1:T(8,128)(2,1)}), bf16[1024,8192]{0,1:T(8,128)(2,1)}) %all-gather.6.cloned.1.call-update) | async-done | bytes 16777232 | tf_op jit(solution)/shard_map/all_gather | solution.py:53
  611.7 10.9 %fusion.10 = (f32[128]{0:T(128)S(1)}, bf16[128,1024]{0,1:T(8,128)(2,1)S(1)}) fusion(bf16[1024,8192]{0,1:T(8,128)(2,1)} %all-gather.6.cloned.1.call-done, bf16[128,8192]{1,0:T(8,128)(2,1)} %all-gather.8.cloned.1.call-done, bf16[128,1024]{0,1:T(8,128)(2,1)S(1)} %copy.27), kind=kOutput, calls=%fused_computation.30 | convolution fusion | flops 2148270080 | bytes 19399168 | tf_op jit(solution)/shard_map/dot_general | solution.py:51
  622.7 21.4 %psum.15 = f32[128]{0:T(128)S(1)} all-reduce(f32[128]{0:T(128)S(1)} %get-tuple-element.23), channel_id=1, replica_groups=mesh['dp'=4,'mp'=8] {'mp'}, use_global_device_ids=true, to_apply=%region_2.4 | all-reduce | flops 128 | bytes 1024 | tf_op jit(solution)/shard_map/psum | solution.py:60
  645.0 45.4 %all-gather.10.cloned.1.call-done = bf16[128,8192]{0,1:T(8,128)(2,1)} async-done(((bf16[128,1024]{0,1:T(8,128)(2,1)}), bf16[128,8192]{0,1:T(8,128)(2,1)}) %all-gather.10.cloned.1.call-update) | async-done | bytes 2097168 | tf_op jit(solution)/shard_map/all_gather | solution.py:65
  690.4 3.9 copy.28
  694.3 3.6 all-to-all-start
  698.2 16.0 %copy.58 = bf16[256,8,2,1792]{3,1,2,0:T(8,128)(2,1)} copy(bf16[256,8,2,1792]{3,2,1,0:T(2,128)(2,1)} %bitcast.78) | data formatting | bytes 29360128
  714.2 9.3 all-to-all-done
  723.6 12.9 %fusion.29 = f32[512,3584]{1,0:T(8,128)} fusion(bf16[512,2048]{1,0:T(8,128)(2,1)S(1)} %bitcast.82, bf16[2048,3584]{1,0:T(8,128)(2,1)} %bitcast.79), kind=kOutput, calls=%fused_computation.65 | convolution fusion | flops 7516192768 | bytes 24117248 | tf_op jit(solution)/shard_map/dot_general | solution.py:71
  736.5 63.7 %reduce-scatter.2.cloned.1.call-done = f32[128,3584]{1,0:T(8,128)} async-done(((f32[512,3584]{1,0:T(8,128)}), f32[128,3584]{1,0:T(8,128)}) %reduce-scatter.2.cloned.1.call-update) | async-done | bytes 1835024 | tf_op jit(solution)/shard_map/reduce_scatter | solution.py:70
  800.3 2.5 fusion.9
  802.8 66.2 %all-gather.12.cloned.1.call-done = bf16[128,14336]{1,0:T(8,128)(2,1)} async-done(((bf16[128,1792]{1,0:T(8,128)(2,1)}), bf16[128,14336]{1,0:T(8,128)(2,1)}) %all-gather.12.cloned.1.call-update) | async-done | bytes 3670032 | tf_op jit(solution)/shard_map/all_gather | solution.py:79
  869.0 4.2 copy.60
  873.2 4.7 all-to-all-start.1
  879.8 6.4 copy.30
  887.1 43.2 %all-to-all-done.1 = bf16[128,4,3584]{2,0,1:T(8,128)(2,1)} async-done(((bf16[128,4,3584]{2,0,1:T(8,128)(2,1)}), bf16[128,4,3584]{2,0,1:T(8,128)(2,1)}, u32[]{:S(2)}, u32[]{:S(2)}) %all-to-all-start.1) | async-done | bytes 3670048 | tf_op jit(solution)/shard_map/all_to_all | solution.py:86
  930.3 14.7 %convolution_multiply_fusion = f32[1792,3584]{1,0:T(8,128)} fusion(bf16[512,1792]{1,0:T(8,128)(2,1)} %all-gather.14.cloned.1.call-done, bf16[512,3584]{1,0:T(8,128)(2,1)} %bitcast.34), kind=kOutput, calls=%fused_computation.1 | convolution fusion | flops 6583091200 | bytes 31195136 | tf_op jit(solution)/shard_map/dot_general | solution.py:88
  (48 shorter events, 15.7 us)
Async XLA Ops:
  8.0 479.9 %all-reduce.2.cloned.1.call-start = ((), (), s32[]{:S(2)}) async-start(), calls=%async_computation.3 | async-start | bytes 1048576 | tf_op jit(solution)/shard_map/psum | solution.py:9
  16.7 7.0 slice-start
  33.2 103.4 %copy-start = (f32[128,2048]{1,0:T(8,128)S(1)}, f32[128,2048]{1,0:T(8,128)}, u32[]{:S(2)}) copy-start(f32[128,2048]{1,0:T(8,128)} %param.13) | copy-start | bytes 3145732
  451.5 54.4 %all-gather.8.cloned.1.call-start = ((), (), s32[]{:S(2)}) async-start(), calls=%async_computation.5 | async-start | bytes 2359296 | tf_op jit(solution)/shard_map/all_gather | solution.py:50
  452.1 159.6 %all-gather.6.cloned.1.call-start = ((), (), s32[]{:S(2)}) async-start(), calls=%async_computation.4 | async-start | bytes 20971520 | tf_op jit(solution)/shard_map/all_gather | solution.py:53
  502.8 0.9 copy-start.1
  502.8 1.1 copy-start.2
  502.9 187.5 %all-gather.10.cloned.1.call-start = ((), (), s32[]{:S(2)}) async-start(), calls=%async_computation.6 | async-start | bytes 2359296 | tf_op jit(solution)/shard_map/all_gather | solution.py:65
  694.3 29.2 %all-to-all-start = ((bf16[128,4,2048]{2,0,1:T(8,128)(2,1)}), bf16[128,4,2048]{2,0,1:T(8,128)(2,1)S(1)}, u32[]{:S(2)}, u32[]{:S(2)}) async-start(bf16[128,4,2048]{2,0,1:T(8,128)(2,1)} %copy.28), calls=%async_computation | async-start | bytes 4194304 | tf_op jit(solution)/shard_map/all_to_all | solution.py:68
  697.9 102.3 %reduce-scatter.2.cloned.1.call-start = ((), (), s32[]{:S(2)}) async-start(), calls=%async_computation.7 | async-start | bytes 9175040 | tf_op jit(solution)/shard_map/reduce_scatter | solution.py:70
  736.5 132.5 %all-gather.12.cloned.1.call-start = ((), (), s32[]{:S(2)}) async-start(), calls=%async_computation.8 | async-start | bytes 4128768 | tf_op jit(solution)/shard_map/all_gather | solution.py:79
  873.2 57.2 %all-to-all-start.1 = ((bf16[128,4,3584]{2,0,1:T(8,128)(2,1)}), bf16[128,4,3584]{2,0,1:T(8,128)(2,1)}, u32[]{:S(2)}, u32[]{:S(2)}) async-start(bf16[128,4,3584]{2,0,1:T(8,128)(2,1)} %bitcast.80), calls=%async_computation.2 | async-start | bytes 7340032 | tf_op jit(solution)/shard_map/all_to_all | solution.py:86
  877.9 52.4 %all-gather.14.cloned.1.call-start = ((), (), s32[]{:S(2)}) async-start(), calls=%async_computation.9 | async-start | bytes 2293760 | tf_op jit(solution)/shard_map/all_gather | solution.py:87
Sparse Core Ops, SparseCore 0:
  451.7 36.1 all-reduce.1
  736.6 63.6 reduce-scatter.1
  880.3 30.1 all-gather.13
Sparse Core Ops, SparseCore 1:
  454.2 51.6 all-gather.7
  507.3 104.3 all-gather.5
  645.1 45.3 all-gather.9
  802.9 66.1 all-gather.11
where the time goes:
time: 954 us; the launch traced here: 952 us
  other arithmetic  437 us (46%)
  waiting for transfers between devices  372 us (39%)
  matrix products  54.6 us (6%)
  local copies, waits for them, and re-layouts  43.5 us (5%)
  blocking collectives  21.4 us (2%)
  between operations  15.6 us (2%)
    another operation x12, other arithmetic, body(): jax.scipy.linalg.solve_triangular(system, target, lower=True, unit_diagon...  421 us
    all_gather x1, waiting for transfers between devices, body(): lax.all_gather(pruned_weight, 'dp', axis=1, tiled=True)  106 us
    all_gather x1, waiting for transfers between devices, body(): hidden_all = lax.all_gather(hidden, 'mp', axis=1, tiled=True)  66.2 us
    reduce_scatter x1, waiting for transfers between devices, body(): lax.psum_scatter(jnp.dot(slices, flat_weight, preferred_element_type=jnp....  63.7 us
    all_gather x1, waiting for transfers between devices, body(): normed_all = lax.all_gather(normed, 'mp', axis=1, tiled=True)  45.4 us
    all_to_all x1, waiting for transfers between devices, body(): lax.all_to_all(hidden_all, 'dp', split_axis=1, concat_axis=0, tiled=True)  43.2 us
    psum x1, waiting for transfers between devices, from_root(): return lax.psum(block, axis)  35.5 us
    unnamed x12, local copies, waits for them, and re-layouts  32 us
  transfers between devices with their start and end apart: 9, of which 8 were waited for; matrix products, arithmetic and copies ran while one was open for 4% of the time, Pallas kernels for 0%

commit v1 on v0

--- a/solution.py
+++ b/solution.py
@@ -76,7 +76,13 @@
     gate_part = gate_up[:, :unit_count]
     up_part = gate_up[:, unit_count:]
     hidden = (jax.nn.silu(gate_part) * up_part).astype(jnp.bfloat16)
-    hidden_all = lax.all_gather(hidden, "mp", axis=1, tiled=True)
+    size = lax.axis_size("mp")
+    held, blocks = (hidden, [hidden])
+    for _ in range(size - 1):
+        held = lax.ppermute(held, "mp", [(i, (i + 1) % size) for i in range(size)])
+        blocks.insert(0, held)
+    line = jnp.concatenate(blocks, axis=1)
+    hidden_all = jnp.roll(line, (lax.axis_index("mp") + 1) * hidden.shape[1], axis=1)
     count_rows = hidden_all.shape[1] // lax.axis_size("mp")
     window_local = lax.dynamic_slice_in_dim(
         hidden_all, lax.axis_index("mp") * count_rows, count_rows, 1

time: 954 us -> 998 us (1.046)
  local copies, waits for them, and re-layouts: 43.5 us -> 65.9 us
  waiting for transfers between devices: 372 us -> 392 us
    ppermute x0 -> x7, waiting for transfers between devices: none -> 86.9 us  [body(): held = lax.ppermute(held, 'mp', [(i, (i + 1) % size) for i in range(size)])]
    all_gather x1 -> x0, waiting for transfers between devices: 66.2 us -> none  [body(): hidden_all = lax.all_gather(hidden, 'mp', axis=1, tiled=True)]
    unnamed x12 -> x38, local copies, waits for them, and re-layouts: 32 us -> 43.4 us
  transfers between devices with their start and end apart: 9 -> 15, of which waited for: 8 -> 14; matrix products, arithmetic and copies ran while one was open for 4% -> 5% of each run, Pallas kernels for 0% -> 0%
where the time goes in v1:
time: 998 us; the launch traced here: 997 us
  other arithmetic  436 us (44%)
  waiting for transfers between devices  392 us (39%)
  local copies, waits for them, and re-layouts  65.9 us (7%)
  matrix products  54.6 us (5%)
  blocking collectives  21.4 us (2%)
  between operations  15.8 us (2%)
  starting transfers between devices  10.8 us (1%)
    another operation x12, other arithmetic, body(): jax.scipy.linalg.solve_triangular(system, target, lower=True, unit_diagon...  421 us
    all_gather x1, waiting for transfers between devices, body(): lax.all_gather(pruned_weight, 'dp', axis=1, tiled=True)  106 us
    ppermute x7, waiting for transfers between devices, body(): held = lax.ppermute(held, 'mp', [(i, (i + 1) % size) for i in range(size)])  86.9 us
    reduce_scatter x1, waiting for transfers between devices, body(): lax.psum_scatter(jnp.dot(slices, flat_weight, preferred_element_type=jnp....  63.8 us
    all_gather x1, waiting for transfers between devices, body(): normed_all = lax.all_gather(normed, 'mp', axis=1, tiled=True)  45.4 us
    unnamed x38, local copies, waits for them, and re-layouts  43.4 us
    all_to_all x1, waiting for transfers between devices, body(): lax.all_to_all(hidden_all, 'dp', split_axis=1, concat_axis=0, tiled=True)  42.8 us
    psum x1, waiting for transfers between devices, from_root(): return lax.psum(block, axis)  35.5 us
  transfers between devices with their start and end apart: 15, of which 14 were waited for; matrix products, arithmetic and copies ran while one was open for 5% of the time, Pallas kernels for 0%

profile of v1, /device:TPU:0, one launch (start us, length us, event | category | flops | bytes accessed | tf_op | source)
XLA Modules:
  0.0 996.8 jit_solution(11041552243087155822)
XLA Ops:
  10.3 6.4 copy.31
  16.7 6.7 convert_element_type.40
  26.0 7.2 add_bitcast_fusion.3
  33.2 100.7 %custom-call.8 = f32[1024,1,32,32]{0,2,3,1:T(8,128)} custom-call(f32[1024,1,32,32]{0,3,2,1:T(8,128)} %get-tuple-element.22), custom_call_target="InvertDiagBlocksLowerTriangular" | custom-call | tf_op jit(solution)/shard_map/jit(_solve_triangular)/vmap()/triangular_solve | solution.py:39
  137.9 100.7 %custom-call.9 = f32[1024,1,32,32]{0,2,3,1:T(8,128)} custom-call(f32[1024,1,32,32]{0,3,2,1:T(8,128)} %get-tuple-element.23), custom_call_target="InvertDiagBlocksLowerTriangular" | custom-call | tf_op jit(solution)/shard_map/jit(_solve_triangular)/vmap()/triangular_solve | solution.py:39
  242.6 100.6 %custom-call.10 = f32[1024,1,32,32]{0,2,3,1:T(8,128)} custom-call(f32[1024,1,32,32]{0,3,2,1:T(8,128)} %get-tuple-element.24), custom_call_target="InvertDiagBlocksLowerTriangular" | custom-call | tf_op jit(solution)/shard_map/jit(_solve_triangular)/vmap()/triangular_solve | solution.py:39
  347.3 100.6 %custom-call.11 = f32[1024,1,32,32]{0,2,3,1:T(8,128)} custom-call(f32[1024,1,32,32]{0,3,2,1:T(8,128)} %get-tuple-element.25), custom_call_target="InvertDiagBlocksLowerTriangular" | custom-call | tf_op jit(solution)/shard_map/jit(_solve_triangular)/vmap()/triangular_solve | solution.py:39
  452.3 35.5 %all-reduce.2.cloned.1.call-done = f32[1024,128]{0,1:T(8,128)} async-done(((f32[1024,128]{0,1:T(8,128)}), f32[1024,128]{0,1:T(8,128)}) %all-reduce.2.cloned.1.call-update) | async-done | bytes 524304 | tf_op jit(solution)/shard_map/psum | solution.py:9
  487.8 12.2 %convolution_subtract_fusion = f32[1024,2048]{0,1:T(8,128)S(1)} fusion(f32[1024,128]{0,1:T(8,128)} %all-reduce.2.cloned.1.call-done, f32[128,2048]{1,0:T(8,128)S(1)} %copy-done.1, bf16[1024,2048]{0,1:T(8,128)(2,1)} %copy.31), kind=kOutput, calls=%fused_computation.2 | convolution fusion | flops 3225419776 | bytes 14155776 | tf_op jit(solution)/shard_map/dot_general | solution.py:45
  505.8 105.8 %all-gather.5.cloned.1.call-done = bf16[1024,8192]{0,1:T(8,128)(2,1)} async-done(((bf16[1024,2048]{0,1:T(8,128)(2,1)}), bf16[1024,8192]{0,1:T(8,128)(2,1)}) %all-gather.5.cloned.1.call-update) | async-done | bytes 16777232 | tf_op jit(solution)/shard_map/all_gather | solution.py:53
  611.7 10.9 %fusion.10 = (f32[128]{0:T(128)S(1)}, bf16[128,1024]{0,1:T(8,128)(2,1)S(1)}) fusion(bf16[1024,8192]{0,1:T(8,128)(2,1)} %all-gather.5.cloned.1.call-done, bf16[128,8192]{1,0:T(8,128)(2,1)} %all-gather.7.cloned.1.call-done, bf16[128,1024]{0,1:T(8,128)(2,1)S(1)} %copy.38), kind=kOutput, calls=%fused_computation.29 | convolution fusion | flops 2148270080 | bytes 19399168 | tf_op jit(solution)/shard_map/dot_general | solution.py:51
  622.6 21.4 %psum.15 = f32[128]{0:T(128)S(1)} all-reduce(f32[128]{0:T(128)S(1)} %get-tuple-element.26), channel_id=1, replica_groups=mesh['dp'=4,'mp'=8] {'mp'}, use_global_device_ids=true, to_apply=%region_2.4 | all-reduce | flops 128 | bytes 1024 | tf_op jit(solution)/shard_map/psum | solution.py:60
  644.9 45.4 %all-gather.9.cloned.1.call-done = bf16[128,8192]{0,1:T(8,128)(2,1)} async-done(((bf16[128,1024]{0,1:T(8,128)(2,1)}), bf16[128,8192]{0,1:T(8,128)(2,1)}) %all-gather.9.cloned.1.call-update) | async-done | bytes 2097168 | tf_op jit(solution)/shard_map/all_gather | solution.py:65
  690.3 3.9 copy.39
  694.2 3.6 all-to-all-start
  698.1 16.0 %copy.69 = bf16[256,8,2,1792]{3,1,2,0:T(8,128)(2,1)} copy(bf16[256,8,2,1792]{3,2,1,0:T(2,128)(2,1)} %bitcast.74) | data formatting | bytes 29360128
  714.2 9.3 all-to-all-done
  723.5 12.9 %fusion.29 = f32[512,3584]{1,0:T(8,128)} fusion(bf16[512,2048]{1,0:T(8,128)(2,1)S(1)} %bitcast.78, bf16[2048,3584]{1,0:T(8,128)(2,1)} %bitcast.75), kind=kOutput, calls=%fused_computation.81 | convolution fusion | flops 7516192768 | bytes 24117248 | tf_op jit(solution)/shard_map/dot_general | solution.py:71
  736.4 63.8 %reduce-scatter.2.cloned.1.call-done = f32[128,3584]{1,0:T(8,128)} async-done(((f32[512,3584]{1,0:T(8,128)}), f32[128,3584]{1,0:T(8,128)}) %reduce-scatter.2.cloned.1.call-update) | async-done | bytes 1835024 | tf_op jit(solution)/shard_map/reduce_scatter | solution.py:70
  803.6 13.3 %collective-permute-done = bf16[128,1792]{1,0:T(8,128)(2,1)S(1)} collective-permute-done((bf16[128,1792]{1,0:T(8,128)(2,1)S(1)}, bf16[128,1792]{1,0:T(8,128)(2,1)S(1)}, u32[]{:S(2)}, u32[]{:S(2)}) %collective-permute-start) | collective-permute-done | bytes 458784 | tf_op jit(solution)/shard_map/ppermute | solution.py:82
  816.9 13.9 %collective-permute-done.1 = bf16[128,1792]{1,0:T(8,128)(2,1)S(1)} collective-permute-done((bf16[128,1792]{1,0:T(8,128)(2,1)S(1)}, bf16[128,1792]{1,0:T(8,128)(2,1)S(1)}, u32[]{:S(2)}, u32[]{:S(2)}) %collective-permute-start.1) | collective-permute-done | bytes 458784 | tf_op jit(solution)/shard_map/ppermute | solution.py:82
  830.9 13.1 %collective-permute-done.2 = bf16[128,1792]{1,0:T(8,128)(2,1)S(1)} collective-permute-done((bf16[128,1792]{1,0:T(8,128)(2,1)S(1)}, bf16[128,1792]{1,0:T(8,128)(2,1)S(1)}, u32[]{:S(2)}, u32[]{:S(2)}) %collective-permute-start.2) | collective-permute-done | bytes 458784 | tf_op jit(solution)/shard_map/ppermute | solution.py:82
  844.0 12.2 %collective-permute-done.3 = bf16[128,1792]{1,0:T(8,128)(2,1)S(1)} collective-permute-done((bf16[128,1792]{1,0:T(8,128)(2,1)S(1)}, bf16[128,1792]{1,0:T(8,128)(2,1)S(1)}, u32[]{:S(2)}, u32[]{:S(2)}) %collective-permute-start.3) | collective-permute-done | bytes 458784 | tf_op jit(solution)/shard_map/ppermute | solution.py:82
  857.0 11.4 %collective-permute-done.4 = bf16[128,1792]{1,0:T(8,128)(2,1)S(1)} collective-permute-done((bf16[128,1792]{1,0:T(8,128)(2,1)S(1)}, bf16[128,1792]{1,0:T(8,128)(2,1)S(1)}, u32[]{:S(2)}, u32[]{:S(2)}) %collective-permute-start.4) | collective-permute-done | bytes 458784 | tf_op jit(solution)/shard_map/ppermute | solution.py:82
  869.1 11.4 %collective-permute-done.5 = bf16[128,1792]{1,0:T(8,128)(2,1)} collective-permute-done((bf16[128,1792]{1,0:T(8,128)(2,1)S(1)}, bf16[128,1792]{1,0:T(8,128)(2,1)}, u32[]{:S(2)}, u32[]{:S(2)}) %collective-permute-start.5) | collective-permute-done | bytes 458784 | tf_op jit(solution)/shard_map/ppermute | solution.py:82
  880.5 11.5 %collective-permute-done.6 = bf16[128,1792]{1,0:T(8,128)(2,1)} collective-permute-done((bf16[128,1792]{1,0:T(8,128)(2,1)}, bf16[128,1792]{1,0:T(8,128)(2,1)}, u32[]{:S(2)}, u32[]{:S(2)}) %collective-permute-start.6) | collective-permute-done | bytes 458784 | tf_op jit(solution)/shard_map/ppermute | solution.py:82
  905.5 6.0 copy.40
  911.6 4.7 all-to-all-start.1
  918.6 6.5 copy.42
  926.0 42.8 %all-to-all-done.1 = bf16[128,4,3584]{0,2,1:T(8,128)(2,1)} async-done(((bf16[128,4,3584]{0,2,1:T(8,128)(2,1)}), bf16[128,4,3584]{0,2,1:T(8,128)(2,1)}, u32[]{:S(2)}, u32[]{:S(2)}) %all-to-all-start.1) | async-done | bytes 3670048 | tf_op jit(solution)/shard_map/all_to_all | solution.py:92
  968.7 6.0 copy.41
  974.7 14.7 %convolution_multiply_fusion = f32[1792,3584]{1,0:T(8,128)} fusion(bf16[512,1792]{1,0:T(8,128)(2,1)} %all-gather.11.cloned.1.call-done, bf16[512,3584]{1,0:T(8,128)(2,1)} %bitcast.77), kind=kOutput, calls=%fused_computation.1 | convolution fusion | flops 6583091200 | bytes 31195136 | tf_op jit(solution)/shard_map/dot_general | solution.py:94
  (89 shorter events, 49.7 us)
Async XLA Ops:
  8.0 479.8 %all-reduce.2.cloned.1.call-start = ((), (), s32[]{:S(2)}) async-start(), calls=%async_computation.3 | async-start | bytes 1048576 | tf_op jit(solution)/shard_map/psum | solution.py:9
  16.7 7.0 slice-start
  33.2 103.4 %copy-start.1 = (f32[128,2048]{1,0:T(8,128)S(1)}, f32[128,2048]{1,0:T(8,128)}, u32[]{:S(2)}) copy-start(f32[128,2048]{1,0:T(8,128)} %param.13) | copy-start | bytes 3145732
  451.5 54.4 %all-gather.7.cloned.1.call-start = ((), (), s32[]{:S(2)}) async-start(), calls=%async_computation.5 | async-start | bytes 2359296 | tf_op jit(solution)/shard_map/all_gather | solution.py:50
  452.1 159.6 %all-gather.5.cloned.1.call-start = ((), (), s32[]{:S(2)}) async-start(), calls=%async_computation.4 | async-start | bytes 20971520 | tf_op jit(solution)/shard_map/all_gather | solution.py:53
  502.8 0.9 copy-start.7
  502.8 1.1 copy-start.8
  502.8 187.5 %all-gather.9.cloned.1.call-start = ((), (), s32[]{:S(2)}) async-start(), calls=%async_computation.6 | async-start | bytes 2359296 | tf_op jit(solution)/shard_map/all_gather | solution.py:65
  694.2 29.2 %all-to-all-start = ((bf16[128,4,2048]{2,0,1:T(8,128)(2,1)}), bf16[128,4,2048]{2,0,1:T(8,128)(2,1)S(1)}, u32[]{:S(2)}, u32[]{:S(2)}) async-start(bf16[128,4,2048]{2,0,1:T(8,128)(2,1)} %copy.39), calls=%async_computation | async-start | bytes 4194304 | tf_op jit(solution)/shard_map/all_to_all | solution.py:68
  697.9 102.3 %reduce-scatter.2.cloned.1.call-start = ((), (), s32[]{:S(2)}) async-start(), calls=%async_computation.7 | async-start | bytes 9175040 | tf_op jit(solution)/shard_map/reduce_scatter | solution.py:70
  800.2 96.4 %copy-start = (f32[128,3584]{1,0:T(8,128)S(1)}, f32[128,3584]{1,0:T(8,128)}, u32[]{:S(2)}) copy-start(f32[128,3584]{1,0:T(8,128)} %reduce-scatter.2.cloned.1.call-done) | copy-start | bytes 5505028
  802.1 14.9 %collective-permute-start = (bf16[128,1792]{1,0:T(8,128)(2,1)S(1)}, bf16[128,1792]{1,0:T(8,128)(2,1)S(1)}, u32[]{:S(2)}, u32[]{:S(2)}) collective-permute-start(bf16[128,1792]{1,0:T(8,128)(2,1)S(1)} %fusion.9), channel_id=1, source_target_pairs={{0,1},{1,2},{2,3},{3,4},{4,5},{5,6},{6,7},{7,0},{8,9},{9,10},{10,1... | collective-permute-start | bytes 1376264 | tf_op jit(solution)/shard_map/ppermute | solution.py:82
  816.9 13.9 %collective-permute-start.1 = (bf16[128,1792]{1,0:T(8,128)(2,1)S(1)}, bf16[128,1792]{1,0:T(8,128)(2,1)S(1)}, u32[]{:S(2)}, u32[]{:S(2)}) collective-permute-start(bf16[128,1792]{1,0:T(8,128)(2,1)S(1)} %collective-permute-done), channel_id=1, source_target_pairs={{0,1},{1,2},{2,3},{3,4},{4,5},{5,6},{6,7},{7,0},{8,9},{9,10},{10,1... | collective-permute-start | bytes 1376264 | tf_op jit(solution)/shard_map/ppermute | solution.py:82
  830.9 13.1 %collective-permute-start.2 = (bf16[128,1792]{1,0:T(8,128)(2,1)S(1)}, bf16[128,1792]{1,0:T(8,128)(2,1)S(1)}, u32[]{:S(2)}, u32[]{:S(2)}) collective-permute-start(bf16[128,1792]{1,0:T(8,128)(2,1)S(1)} %collective-permute-done.1), channel_id=1, source_target_pairs={{0,1},{1,2},{2,3},{3,4},{4,5},{5,6},{6,7},{7,0},{8,9},{9,10},{10,1... | collective-permute-start | bytes 1376264 | tf_op jit(solution)/shard_map/ppermute | solution.py:82
  844.0 12.2 %collective-permute-start.3 = (bf16[128,1792]{1,0:T(8,128)(2,1)S(1)}, bf16[128,1792]{1,0:T(8,128)(2,1)S(1)}, u32[]{:S(2)}, u32[]{:S(2)}) collective-permute-start(bf16[128,1792]{1,0:T(8,128)(2,1)S(1)} %collective-permute-done.2), channel_id=1, source_target_pairs={{0,1},{1,2},{2,3},{3,4},{4,5},{5,6},{6,7},{7,0},{8,9},{9,10},{10,1... | collective-permute-start | bytes 1376264 | tf_op jit(solution)/shard_map/ppermute | solution.py:82
  856.2 0.8 copy-start.3
  857.0 11.4 %collective-permute-start.4 = (bf16[128,1792]{1,0:T(8,128)(2,1)S(1)}, bf16[128,1792]{1,0:T(8,128)(2,1)S(1)}, u32[]{:S(2)}, u32[]{:S(2)}) collective-permute-start(bf16[128,1792]{1,0:T(8,128)(2,1)S(1)} %collective-permute-done.3), channel_id=1, source_target_pairs={{0,1},{1,2},{2,3},{3,4},{4,5},{5,6},{6,7},{7,0},{8,9},{9,10},{10,1... | collective-permute-start | bytes 1376264 | tf_op jit(solution)/shard_map/ppermute | solution.py:82
  868.3 0.8 copy-start.5
  869.1 11.4 %collective-permute-start.5 = (bf16[128,1792]{1,0:T(8,128)(2,1)S(1)}, bf16[128,1792]{1,0:T(8,128)(2,1)}, u32[]{:S(2)}, u32[]{:S(2)}) collective-permute-start(bf16[128,1792]{1,0:T(8,128)(2,1)S(1)} %collective-permute-done.4), channel_id=1, source_target_pairs={{0,1},{1,2},{2,3},{3,4},{4,5},{5,6},{6,7},{7,0},{8,9},{9,10},{10,1... | collective-permute-start | bytes 1376264 | tf_op jit(solution)/shard_map/ppermute | solution.py:82
  880.5 11.5 %collective-permute-start.6 = (bf16[128,1792]{1,0:T(8,128)(2,1)}, bf16[128,1792]{1,0:T(8,128)(2,1)}, u32[]{:S(2)}, u32[]{:S(2)}) collective-permute-start(bf16[128,1792]{1,0:T(8,128)(2,1)} %collective-permute-done.5), channel_id=1, source_target_pairs={{0,1},{1,2},{2,3},{3,4},{4,5},{5,6},{6,7},{7,0},{8,9},{9,10},{10,1... | collective-permute-start | bytes 1376264 | tf_op jit(solution)/shard_map/ppermute | solution.py:82
  894.1 4.8 copy-start.6
  895.3 3.7 copy-start.4
  899.5 3.1 copy-start.2
  911.6 57.2 %all-to-all-start.1 = ((bf16[128,4,3584]{0,2,1:T(8,128)(2,1)}), bf16[128,4,3584]{0,2,1:T(8,128)(2,1)}, u32[]{:S(2)}, u32[]{:S(2)}) async-start(bf16[128,4,3584]{0,2,1:T(8,128)(2,1)} %bitcast.76), calls=%async_computation.2 | async-start | bytes 7340032 | tf_op jit(solution)/shard_map/all_to_all | solution.py:92
  916.3 58.4 %all-gather.11.cloned.1.call-start = ((), (), s32[]{:S(2)}) async-start(), calls=%async_computation.8 | async-start | bytes 2293760 | tf_op jit(solution)/shard_map/all_gather | solution.py:93
Sparse Core Ops, SparseCore 0:
  451.6 36.1 all-reduce.1
  736.5 63.6 reduce-scatter.1
  918.8 28.6 all-gather.10
Sparse Core Ops, SparseCore 1:
  454.2 51.6 all-gather.6
  507.3 104.3 all-gather.4
  645.0 45.3 all-gather.8
